TPU v7x, 32 devices: a whole 2x2x4 slice. The times are simulated.
32 devices in a mesh: grp: 4 (over z), dev: 8 (over y, x, core).
Axes of the slice: x: 2, y: 2, z: 4, core: 2. Of those that a mesh axis runs over, the one named last changes fastest.
Arguments:
- images: bfloat16 [1536, 1536], P(('grp', 'dev')), may hold values from -1 to 1, as said below
- texts: bfloat16 [1536, 1536], P(('grp', 'dev')), may hold values from -1 to 1, as said below
- logit_scale: float32 [1], replicated, may hold values from 20 to 60
- logit_bias: float32 [1], replicated, may hold values from -12 to -8
Outputs:
- grad_image: float32 [1536, 1536], P(('grp', 'dev'))
- grad_text: float32 [1536, 1536], P(('grp', 'dev'))
- loss: float32 [1], replicated
Inputs may be any that keep to these rules, and one draw needn't show every extreme that they name: `images`: every row has length 1 up to bfloat16 rounding. `texts`: every row has length 1 up to bfloat16 rounding.
All inputs are finite; a program needn't handle non-finite values.
Results may differ from a plain program's by a relative error of at most 0.00095.
Values may be sent and summed in bfloat16 or wider, within the bound.
A program may use at most 128 MiB of HBM per device.

v0:
```python
import functools
import math

import jax
import jax.numpy as jnp
from jax import lax
from jax.experimental import pallas as pl
from jax.experimental.pallas import tpu as pltpu
from jax.sharding import PartitionSpec as P

MESH = pl.DeviceIdType.MESH
CORES = 2


def split_chips(members):
    chips = members // CORES
    q_size = math.isqrt(chips)
    while chips % q_size:
        q_size -= 1
    return chips // q_size, q_size


def piece_count(rows):
    for pieces in (3, 2):
        if rows % (16 * pieces) == 0:
            return pieces
    return 1


def pair_terms(logits, matched):
    small = jnp.exp(-jnp.abs(logits))
    sigmoid = jnp.where(logits >= 0, 1.0, small) / (1.0 + small)
    if matched is None:
        return sigmoid, jnp.maximum(logits, 0.0) + jnp.log1p(small)
    weights = sigmoid - matched.astype(jnp.float32)
    signed = jnp.where(matched, -logits, logits)
    return weights, jnp.maximum(signed, 0.0) + jnp.log1p(small)


def kernel(
    groups, p_size, q_size, pieces,
    img_hbm, txt_hbm, scale_hbm, bias_hbm,
    gi_ref, gt_ref, loss_ref,
    img_all, txt_all, acc_i, acc_t, part_i, part_t,
    loss_acc, loss_own, loss_dev, loss_sum, loss_grp,
    img_recv, img_z, img_plane, img_core,
    txt_recv, txt_z, txt_plane, txt_core,
    pi_send, pi_recv, pt_send, pt_recv,
    ld_send, ld_recv, lg_send, lg_recv,
    scale_ref, bias_ref, fetch_sem,
):
    rows = img_hbm.shape[0]
    members = p_size * q_size * CORES
    g = lax.axis_index("grp")
    d = lax.axis_index("dev")
    c = lax.rem(d, CORES)
    chip = d // CORES
    q = lax.rem(chip, q_size)
    p = chip // q_size
    step_rows = rows // pieces

    def member(pi, qi, ci):
        return (pi * q_size + qi) * CORES + ci

    fetches = [
        pltpu.make_async_copy(src, dst, fetch_sem.at[i])
        for i, (src, dst) in enumerate((
            (txt_hbm, txt_all.at[g, q, c]), (img_hbm, img_all.at[g, p, c]), (scale_hbm, scale_ref), (bias_hbm, bias_ref),
        ))
    ]
    barrier = pltpu.get_barrier_semaphore()

    def greet(axis, index):
        pl.semaphore_signal(barrier, inc=1, device_id={axis: index}, device_id_type=MESH)

    @pl.when(g + 1 < groups)
    def _():
        greet("grp", g + 1)

    @pl.when(g > 0)
    def _():
        greet("grp", g - 1)

    for k in range(1, p_size):
        greet("dev", member(lax.rem(p + k, p_size), q, c))
    for k in range(1, q_size):
        greet("dev", member(p, lax.rem(q + k, q_size), c))
    greet("dev", member(p, q, 1 - c))
    for fetch in fetches:
        fetch.start()
    edges = (g > 0).astype(jnp.int32) + (g + 1 < groups).astype(jnp.int32)
    pl.semaphore_wait(barrier, p_size + q_size - 1 + edges)

    class Side:
        def __init__(self, all_ref, recv, zs, ps, cs, me, size, partner):
            self.all, self.recv = all_ref, recv
            self.zs, self.ps, self.cs = zs, ps, cs
            self.me, self.size, self.partner = me, size, partner

        def piece(self, gg, m, cc, h):
            return self.all.at[gg, m, cc, pl.ds(h * step_rows, step_rows)]

        def copy(self, gg, m, cc, h, send, target):
            dst = self.piece(gg, m, cc, h)
            return pltpu.make_async_remote_copy(
                src_ref=dst, dst_ref=dst, send_sem=send, recv_sem=self.recv.at[gg, m, cc, h],
                device_id=target, device_id_type=MESH,
            )

        def arrived(self, gg, m, cc, h):
            self.copy(gg, m, cc, h, self.cs.at[0, 0, 0], {"dev": member(p, q, 1 - c)}).wait_recv()

        def along_z(self, gg, h, up, own=False):
            slot = gg if (up or not own) else groups
            return self.copy(gg, self.me, c, h, self.zs.at[slot, h], {"grp": g + 1 if up else g - 1})

        def to_plane(self, gg, k, h):
            other = lax.rem(self.me + k, self.size)
            return self.copy(gg, self.me, c, h, self.ps.at[gg, k - 1, h], {"dev": self.partner(other)})

        def to_core(self, gg, m, h):
            return self.copy(gg, m, c, h, self.cs.at[gg, m, h], {"dev": member(p, q, 1 - c)})

    texts = Side(txt_all, txt_recv, txt_z, txt_plane, txt_core, q, q_size, lambda o: member(p, o, c))
    images = Side(img_all, img_recv, img_z, img_plane, img_core, p, p_size, lambda o: member(o, q, c))
    sides = (texts, images)

    def from_side(s, down):
        return (g - s, g >= s) if not down else (g + s, g + s < groups)

    for side, fetch in zip(sides, fetches):
        fetch.wait()
        for h in range(pieces):
            @pl.when(g + 1 < groups)
            def _():
                side.along_z(g, h, True, True).start()

            @pl.when(g > 0)
            def _():
                side.along_z(g, h, False, True).start()

            for k in range(1, side.size):
                side.to_plane(g, k, h).start()
            side.to_core(g, side.me, h).start()
    for fetch in fetches[2:]:
        fetch.wait()
    multiplier = scale_ref[0]
    offset = bias_ref[0]

    def forward_z(s, side):
        for h in range(pieces):
            for down in (False, True):
                gg, there = from_side(s, down)

                @pl.when(there)
                def _():
                    side.arrived(gg, side.me, c, h)

                    @pl.when((g > 0) if down else (g + 1 < groups))
                    def _():
                        side.along_z(gg, h, not down).start()

                    for k in range(1, side.size):
                        side.to_plane(gg, k, h).start()
                    side.to_core(gg, side.me, h).start()

    def each_chunk(s, act):
        if s == 0:
            act(g)
            return
        for down in (False, True):
            gg, there = from_side(s, down)

            @pl.when(there)
            def _():
                act(gg)

    def relay_plane(s, side):
        def act(gg):
            for h in range(pieces):
                for k in range(1, side.size):
                    other = lax.rem(side.me + k, side.size)
                    side.arrived(gg, other, c, h)
                    side.to_core(gg, other, h).start()

        each_chunk(s, act)

    def gradient(mine, other, acc, gg, first, losses):
        width = acc.shape[2]
        left = mine.all[g, :, c].reshape(mine.size * rows, width)
        right = other.all[gg].reshape(other.size * CORES * rows, width)
        logits = lax.dot_general(left, right, (((1,), (1,)), ((), ())), preferred_element_type=jnp.float32)
        logits = logits * multiplier + offset
        matched = None
        if first:
            row = lax.broadcasted_iota(jnp.int32, logits.shape, 0) - mine.me * rows
            col = lax.broadcasted_iota(jnp.int32, logits.shape, 1) - (other.me * CORES + c) * rows
            matched = (row == col) & (row >= 0) & (row < rows)
        weights, terms = pair_terms(logits, matched)
        if losses:
            loss_acc[...] = terms if first else loss_acc[...] + terms
        product = jnp.dot(weights.astype(jnp.bfloat16), right, preferred_element_type=jnp.float32)
        product = product.reshape(mine.size, rows, width)
        acc[...] = product if first else acc[...] + product

    def compute(s, mine, other, acc, losses):
        def act(gg):
            for m in range(other.size):
                for h in range(pieces):
                    other.arrived(gg, m, 1 - c, h)
            gradient(mine, other, acc, gg, s == 0, losses)

        each_chunk(s, act)

    def partial(acc, part, send, recv, side, k):
        other = lax.rem(side.me + k, side.size)
        return pltpu.make_async_remote_copy(
            src_ref=acc.at[other], dst_ref=part.at[side.me], send_sem=send.at[k - 1], recv_sem=recv.at[side.me],
            device_id={"dev": side.partner(other)}, device_id_type=MESH,
        )

    def partial_in(acc, part, send, recv, side, k):
        other = lax.rem(side.me + k, side.size)
        return pltpu.make_async_remote_copy(
            src_ref=acc.at[other], dst_ref=part.at[other], send_sem=send.at[k - 1], recv_sem=recv.at[other],
            device_id={"dev": side.partner(other)}, device_id_type=MESH,
        )

    def send_partials(acc, part, send, recv, side):
        for k in range(1, side.size):
            partial(acc, part, send, recv, side, k).start()

    def loss_copy(own, gathered, send, recv, axis, me, size, k, slot):
        return pltpu.make_async_remote_copy(
            src_ref=own, dst_ref=gathered.at[slot], send_sem=send.at[k - 1], recv_sem=recv.at[slot],
            device_id={axis: lax.rem(me + k, size)}, device_id_type=MESH,
        )

    def loss_out(value, own, gathered, send, recv, axis, me, size):
        own[...] = value
        gathered[me] = value
        for k in range(1, size):
            loss_copy(own, gathered, send, recv, axis, me, size, k, me).start()

    def loss_in(own, gathered, send, recv, axis, me, size):
        for k in range(1, size):
            loss_copy(own, gathered, send, recv, axis, me, size, k, lax.rem(me + k, size)).wait_recv()
        total = gathered[0]
        for k in range(1, size):
            total = total + gathered[k]
        return total

    over_dev = (loss_own, loss_dev, ld_send, ld_recv, "dev", d, members)
    over_grp = (loss_sum, loss_grp, lg_send, lg_recv, "grp", g, groups)
    text_part = (acc_t, part_t, pt_send, pt_recv, texts)
    image_part = (acc_i, part_i, pi_send, pi_recv, images)

    last = groups - 1
    for s in range(1, groups):
        forward_z(s, texts)
        forward_z(s, images)
        relay_plane(s - 1, texts)
        relay_plane(s - 1, images)
        compute(s - 1, images, texts, acc_i, True)
        compute(s - 1, texts, images, acc_t, False)
    relay_plane(last, texts)
    relay_plane(last, images)
    compute(last, images, texts, acc_i, True)
    loss_out(jnp.full((8, 128), jnp.sum(loss_acc[...]), jnp.float32), *over_dev)
    send_partials(*image_part)
    compute(last, texts, images, acc_t, False)
    send_partials(*text_part)
    loss_out(loss_in(*over_dev), *over_grp)
    loss_ref[...] = loss_in(*over_grp) * (1.0 / (rows * members * groups))

    for (acc, part, send, recv, side), out_ref in ((image_part, gi_ref), (text_part, gt_ref)):
        total = acc[side.me]
        for k in range(1, side.size):
            partial_in(acc, part, send, recv, side, k).wait_recv()
            total = total + part[lax.rem(side.me + k, side.size)]
        out_ref[...] = multiplier * total
        for k in range(1, side.size):
            partial(acc, part, send, recv, side, k).wait_send()
    for own, gathered, send, recv, axis, me, size in (over_dev, over_grp):
        for k in range(1, size):
            loss_copy(own, gathered, send, recv, axis, me, size, k, me).wait_send()

    for side in sides:
        for h in range(pieces):
            @pl.when(g + 1 < groups)
            def _():
                side.along_z(g, h, True, True).wait_send()

            @pl.when(g > 0)
            def _():
                side.along_z(g, h, False, True).wait_send()

            for s in range(groups):
                def act(gg):
                    for k in range(1, side.size):
                        side.to_plane(gg, k, h).wait_send()
                    for m in range(side.size):
                        side.to_core(gg, m, h).wait_send()

                each_chunk(s, act)
                for down in (False, True):
                    if s:
                        gg, there = from_side(s, down)

                        @pl.when(there & ((g > 0) if down else (g + 1 < groups)))
                        def _():
                            side.along_z(gg, h, not down).wait_send()


def write_out(gi_ref, gt_ref, loss_ref, gi_out, gt_out, loss_out):
    gi_out[...] = gi_ref[...]
    gt_out[...] = gt_ref[...]
    loss_out[0] = jnp.max(loss_ref[...])


def shards(groups, members, images, texts, logit_scale, logit_bias):
    rows, width = images.shape
    p_size, q_size = split_chips(members)
    pieces = piece_count(rows)
    f32, bf16 = jnp.float32, jnp.bfloat16
    dma = pltpu.SemaphoreType.DMA

    def side_sems(size):
        return [
            dma((groups, size, CORES, pieces)),
            dma((groups + 1, pieces)),
            dma((groups, max(size - 1, 1), pieces)),
            dma((groups, size, pieces)),
        ]

    held = (groups * (p_size + q_size) * CORES * 2 + (p_size + q_size) * 8) * rows * width
    vmem, smem = pl.BlockSpec(memory_space=pltpu.VMEM), pl.BlockSpec(memory_space=pltpu.SMEM)
    grad_image, grad_text, loss = pl.pallas_call(
        functools.partial(kernel, groups, p_size, q_size, pieces),
        out_shape=(
            jax.ShapeDtypeStruct((rows, width), f32),
            jax.ShapeDtypeStruct((rows, width), f32),
            jax.ShapeDtypeStruct((8, 128), f32),
        ),
        in_specs=[pl.BlockSpec(memory_space=pl.ANY)] * 4,
        out_specs=(vmem, vmem, vmem),
        scratch_shapes=[
            pltpu.VMEM((groups, p_size, CORES, rows, width), bf16),
            pltpu.VMEM((groups, q_size, CORES, rows, width), bf16),
            pltpu.VMEM((p_size, rows, width), f32),
            pltpu.VMEM((q_size, rows, width), f32),
            pltpu.VMEM((p_size, rows, width), f32),
            pltpu.VMEM((q_size, rows, width), f32),
            pltpu.VMEM((p_size * rows, q_size * CORES * rows), f32),
            pltpu.VMEM((8, 128), f32),
            pltpu.VMEM((members, 8, 128), f32),
            pltpu.VMEM((8, 128), f32),
            pltpu.VMEM((groups, 8, 128), f32),
            *side_sems(p_size),
            *side_sems(q_size),
            dma((p_size,)), dma((p_size,)), dma((q_size,)), dma((q_size,)),
            dma((members,)), dma((members,)), dma((groups,)), dma((groups,)),
            pltpu.SMEM((1,), f32), pltpu.SMEM((1,), f32), dma((4,)),
        ],
        compiler_params=pltpu.CompilerParams(
            collective_id=0, has_side_effects=True, vmem_limit_bytes=min(held + (members + groups) * 4096 + (12 << 20), 60 << 20)
        ),
    )(pltpu.with_memory_space_constraint(images, pltpu.HBM), pltpu.with_memory_space_constraint(texts, pltpu.HBM), logit_scale, logit_bias)
    return pl.pallas_call(
        write_out,
        out_shape=(
            jax.ShapeDtypeStruct((rows, width), f32),
            jax.ShapeDtypeStruct((rows, width), f32),
            jax.ShapeDtypeStruct((1,), f32),
        ),
        in_specs=[vmem, vmem, vmem],
        out_specs=(vmem, vmem, smem),
        compiler_params=pltpu.CompilerParams(vmem_limit_bytes=4 << 20),
    )(grad_image, grad_text, loss)


def solution(mesh):
    in_specs = (P(("grp", "dev"), None), P(("grp", "dev"), None), P(), P())
    out_specs = (P(("grp", "dev"), None), P(("grp", "dev"), None), P())
    body = functools.partial(shards, mesh.shape["grp"], mesh.shape["dev"])
    return jax.shard_map(body, mesh=mesh, in_specs=in_specs, out_specs=out_specs, check_vma=False)
```

profile of v0, /device:TPU:0, one launch (start us, length us, event | category | flops | bytes accessed | tf_op | source)
XLA Modules:
  0.0 43.5 jit_solution(2492184468159872502)
XLA Ops:
  1.9 40.7 %shard_map.67 = (f32[48,1536]{1,0:T(8,128)S(1)}, f32[48,1536]{1,0:T(8,128)S(1)}, f32[8,128]{1,0:T(8,128)S(1)}) custom-call(bf16[48,1536]{1,0:T(8,128)(2,1)} %img_hbm.1, bf16[48,1536]{1,0:T(8,128)(2,1)} %txt_hbm.1, f32[1]{0:T(128)S(6)} %copy.7.scale_hbm, f32[1]{0:T(128)S(6)} %copy.8.bias_hbm), custom_call_target="tpu_custom_call" | custom-call | tf_op jit(solution)/shard_map/pallas_call | solution.py:338
  42.6 0.8 %shard_map.68 = (f32[48,1536]{1,0:T(8,128)}, f32[48,1536]{1,0:T(8,128)}, f32[1]{0:T(128)}) custom-call(f32[48,1536]{1,0:T(8,128)S(1)} %get-tuple-element.6.gi_ref, f32[48,1536]{1,0:T(8,128)S(1)} %get-tuple-element.7.gt_ref, f32[8,128]{1,0:T(8,128)S(1)} %get-tuple-element.8.loss_ref), custom_call_target="tpu_custom_call" | custom-call | tf_op jit(solution)/shard_map/pallas_call | solution.py:369
where the time goes:
time: 43.6 us; the launch traced here: 43.5 us
  Pallas kernels  41.5 us (95%)
  between operations  1.93 us (4%)
    pallas_call x1, Pallas kernels, shards(): pl.pallas_call(functools.partial(kernel, groups, p_size, q_size, pieces),...  40.7 us

commit v1 on v0

v1 whole, which is shorter than its diff:
```python
import functools
import math

import jax
import jax.numpy as jnp
from jax import lax
from jax.experimental import pallas as pl
from jax.experimental.pallas import tpu as pltpu
from jax.sharding import PartitionSpec as P

MESH = pl.DeviceIdType.MESH
CORES = 2
POWER = 5


def split_chips(members):
    chips = members // CORES
    q_size = math.isqrt(chips)
    while chips % q_size:
        q_size -= 1
    return chips // q_size, q_size


def split_groups(groups):
    sets = math.isqrt(groups)
    while groups % sets:
        sets -= 1
    return sets, groups // sets


def piece_count(rows):
    for pieces in (3, 2):
        if rows % (16 * pieces) == 0:
            return pieces
    return 1


def pair_terms(logits, matched, losses):
    small = jnp.exp(-jnp.abs(logits))
    sigmoid = jnp.where(logits >= 0, 1.0, small) / (1.0 + small)
    weights = sigmoid - matched.astype(jnp.float32)
    if not losses:
        return weights, None
    signed = jnp.where(matched, -logits, logits)
    return weights, jnp.maximum(signed, 0.0) + jnp.log1p(small)


def encode(values, unit):
    scaled = values * unit
    square = scaled * scaled
    return (square * square * scaled).astype(jnp.bfloat16)


def decode(codes, unit):
    codes = codes.astype(jnp.float32)
    size = jnp.exp(jnp.log(jnp.abs(codes)) * (1.0 / POWER)) * (1.0 / unit)
    return jnp.where(codes < 0, -size, size)


def kernel(
    t_sets, i_sets, p_size, q_size, pieces, unit,
    img_hbm, txt_hbm, scale_ref, bias_ref,
    gi_ref, gt_ref, loss_ref,
    img_all, txt_all, acc_i, acc_t, code_i, code_t, part_i, part_t,
    zs_i, zs_t, zr_i, zr_t,
    loss_acc, loss_own, loss_dev, loss_sum, loss_set, loss_all, loss_grp,
    img_recv, img_z, img_plane, img_core,
    txt_recv, txt_z, txt_plane, txt_core,
    pi_send, pi_recv, pt_send, pt_recv,
    zi_send, zi_recv, zt_send, zt_recv,
    ld_send, ld_recv, ls_send, ls_recv, lg_send, lg_recv,
    fetch_sem,
):
    rows, width = img_hbm.shape
    members = p_size * q_size * CORES
    i_count, t_count = t_sets, i_sets
    groups = i_sets * t_sets
    g = lax.axis_index("grp")
    d = lax.axis_index("dev")
    c = lax.rem(d, CORES)
    chip = d // CORES
    q = lax.rem(chip, q_size)
    p = chip // q_size
    a = g // t_sets
    b = lax.rem(g, t_sets)
    home = g // t_count
    step_rows = rows // pieces

    def member(pi, qi, ci):
        return (pi * q_size + qi) * CORES + ci

    def img_group(k):
        return a * i_count + k

    def txt_group(j):
        return b * t_count + j

    t_own = home == b
    t_slot = lax.rem(g, t_count)
    t_place = jnp.where(t_own, t_slot, t_count)
    below, above = home > b, home < b
    t_first = jnp.where(t_own, t_slot, jnp.where(below, t_count - 1, 0))
    t_turn = jnp.where(below, t_count - 1, 1)
    t_order = [lax.rem(t_first + i * t_turn, t_count) for i in range(t_count)]
    i_order = [lax.rem(b + i, i_count) for i in range(i_count)]

    started = []

    def start(make, when=None):
        started.append((make, when))
        if when is None:
            make().start()
        else:
            pl.when(when)(lambda: make().start())

    def remote(src, dst, send, recv, target):
        return pltpu.make_async_remote_copy(
            src_ref=src, dst_ref=dst, send_sem=send, recv_sem=recv, device_id=target, device_id_type=MESH,
        )

    fetches = [
        pltpu.make_async_copy(src, dst, fetch_sem.at[i])
        for i, (src, dst) in enumerate((
            (txt_hbm, txt_all.at[t_place, q, c]), (img_hbm, img_all.at[b, p, c]),
        ))
    ]
    for fetch in fetches:
        fetch.start()
    barrier = pltpu.get_barrier_semaphore()

    def greet(axis, index):
        pl.semaphore_signal(barrier, inc=1, device_id={axis: index}, device_id_type=MESH)

    def txt_target(i):
        return i * t_sets + home

    awaited = (i_count - 1) + (p_size - 1) + (q_size - 1) + 1
    for i in range(1, i_count):
        greet("grp", img_group(i_order[i]))
    for j in range(t_count):
        pl.when(txt_group(j) != g)(functools.partial(lambda j: greet("grp", txt_group(j)), j))
    for i in range(i_sets):
        awaited = awaited + (txt_target(i) != g).astype(jnp.int32)
    for k in range(1, p_size):
        greet("dev", member(lax.rem(p + k, p_size), q, c))
    for k in range(1, q_size):
        greet("dev", member(p, lax.rem(q + k, q_size), c))
    greet("dev", member(p, q, 1 - c))
    pl.semaphore_wait(barrier, awaited)

    class Side:
        def __init__(self, all_ref, recv, zs, ps, cs, me, size, partner):
            self.all, self.recv = all_ref, recv
            self.zs, self.ps, self.cs = zs, ps, cs
            self.me, self.size, self.partner = me, size, partner

        def piece(self, n, m, cc, h):
            return self.all.at[n, m, cc, pl.ds(h * step_rows, step_rows)]

        def arrived(self, n, m, cc, h):
            ref = self.piece(n, m, cc, h)
            remote(ref, ref, self.cs.at[0, 0, 0], self.recv.at[n, m, cc, h], {"dev": member(p, q, 1 - c)}).wait_recv()

        def out(self, n, m, h, send, target, source=None):
            ref = self.piece(n, m, c, h)
            src = ref if source is None else self.piece(source, m, c, h)
            return remote(src, ref, send, self.recv.at[n, m, c, h], target)

        def spread(self, n, h, when=None):
            for k in range(1, self.size):
                other = lax.rem(self.me + k, self.size)
                start(lambda k=k, other=other: self.out(n, self.me, h, self.ps.at[n, k - 1, h], {"dev": self.partner(other)}), when)
            self.pass_on(n, self.me, h, when)

        def pass_on(self, n, m, h, when=None):
            start(lambda: self.out(n, m, h, self.cs.at[n, m, h], {"dev": member(p, q, 1 - c)}), when)

        def relay(self, n, h, own=None):
            if own is None:
                self.arrived(n, self.me, c, h)
            else:
                pl.when(jnp.logical_not(own))(lambda: self.arrived(n, self.me, c, h))
            self.spread(n, h)

        def relay_plane(self, n, h):
            for k in range(1, self.size):
                other = lax.rem(self.me + k, self.size)
                self.arrived(n, other, c, h)
                self.pass_on(n, other, h)

        def complete(self, n):
            for m in range(self.size):
                for h in range(pieces):
                    self.arrived(n, m, 1 - c, h)

    texts = Side(txt_all, txt_recv, txt_z, txt_plane, txt_core, q, q_size, lambda o: member(p, o, c))
    images = Side(img_all, img_recv, img_z, img_plane, img_core, p, p_size, lambda o: member(o, q, c))

    fetches[0].wait()
    for h in range(pieces):
        for i in range(i_sets):
            start(
                lambda i=i, h=h: texts.out(t_slot, q, h, txt_z.at[i, h], {"grp": txt_target(i)}, t_place),
                txt_target(i) != g,
            )
    fetches[1].wait()
    for h in range(pieces):
        for i in range(1, i_count):
            start(lambda i=i, h=h: images.out(b, p, h, img_z.at[i, h], {"grp": img_group(i_order[i])}))
        images.spread(b, h)
    multiplier = scale_ref[0]
    offset = bias_ref[0]

    for h in range(pieces):
        texts.relay(t_order[0], h, t_own)
    for h in range(pieces):
        images.relay_plane(b, h)
    for h in range(pieces):
        for i in range(1, i_count):
            images.relay(i_order[i], h)
        for i in range(1, t_count):
            texts.relay(t_order[i], h)
        texts.relay_plane(t_order[0], h)
    for h in range(pieces):
        for i in range(1, t_count):
            texts.relay_plane(t_order[i], h)
        for i in range(1, i_count):
            images.relay_plane(i_order[i], h)

    def weigh(left, right, row_start, col_start, losses):
        logits = lax.dot_general(left, right, (((1,), (1,)), ((), ())), preferred_element_type=jnp.float32)
        logits = logits * multiplier + offset
        row = lax.broadcasted_iota(jnp.int32, logits.shape, 0) - row_start
        col = lax.broadcasted_iota(jnp.int32, logits.shape, 1) - col_start
        matched = (row == col) & (row >= 0) & (row < rows)
        weights, terms = pair_terms(logits, matched, losses)
        return jnp.dot(weights.astype(jnp.bfloat16), right, preferred_element_type=jnp.float32), terms

    far = 1 << 24

    def image_pass(k, first):
        left = img_all[k, :, c].reshape(p_size * rows, width)
        right = txt_all[0:t_count].reshape(t_count * q_size * CORES * rows, width)
        j = img_group(k) - b * t_count
        col = jnp.where((j >= 0) & (j < t_count), ((j * q_size + q) * CORES + c) * rows, far)
        product, terms = weigh(left, right, p * rows, col, True)
        loss_acc[...] = terms if first else loss_acc[...] + terms
        acc_i[k] = product.reshape(p_size, rows, width)

    def text_pass(j):
        left = txt_all[j, :, c].reshape(q_size * rows, width)
        right = img_all[...].reshape(i_count * p_size * CORES * rows, width)
        k = txt_group(j) - a * i_count
        col = jnp.where((k >= 0) & (k < i_count), ((k * p_size + p) * CORES + c) * rows, far)
        product, _ = weigh(left, right, q * rows, col, False)
        acc_t[j] = product.reshape(q_size, rows, width)

    def part(acc, code, recv_buf, send, recv, side, n, k, h):
        other = lax.rem(side.me + k, side.size)
        window = pl.ds(h * step_rows, step_rows)
        return remote(
            code.at[n, k - 1, window], recv_buf.at[n, side.me, window], send.at[n, k - 1, h], recv.at[n, side.me, h],
            {"dev": side.partner(other)},
        )

    def send_parts(acc, code, recv_buf, send, recv, side, n):
        for h in range(pieces):
            window = pl.ds(h * step_rows, step_rows)
            for k in range(1, side.size):
                other = lax.rem(side.me + k, side.size)
                code[n, k - 1, window] = encode(acc[n, other, window], unit)
                start(lambda k=k, h=h: part(acc, code, recv_buf, send, recv, side, n, k, h))

    def sum_parts(acc, code, recv_buf, send, recv, side, n, h):
        window = pl.ds(h * step_rows, step_rows)
        total = acc[n, side.me, window]
        for k in range(1, side.size):
            other = lax.rem(side.me + k, side.size)
            ref = recv_buf.at[n, other, window]
            remote(ref, ref, send.at[0, 0, 0], recv.at[n, other, h], {"dev": side.partner(other)}).wait_recv()
            total = total + decode(recv_buf[n, other, window], unit)
        return total

    image_parts = (acc_i, code_i, part_i, pi_send, pi_recv, images)
    text_parts = (acc_t, code_t, part_t, pt_send, pt_recv, texts)

    def loss_copy(own, gathered, send, recv, target, me, size, k, slot):
        return remote(own, gathered.at[slot], send.at[k - 1], recv.at[slot], target(lax.rem(me + k, size)))

    def loss_out(value, own, gathered, send, recv, target, me, size):
        own[...] = value
        gathered[me] = value
        for k in range(1, size):
            start(lambda k=k: loss_copy(own, gathered, send, recv, target, me, size, k, me))

    def loss_in(own, gathered, send, recv, target, me, size):
        for k in range(1, size):
            loss_copy(own, gathered, send, recv, target, me, size, k, lax.rem(me + k, size)).wait_recv()
        total = gathered[0]
        for k in range(1, size):
            total = total + gathered[k]
        return total

    over_dev = (loss_own, loss_dev, ld_send, ld_recv, lambda o: {"dev": o}, d, members)
    over_set = (loss_sum, loss_set, ls_send, ls_recv, lambda o: {"grp": a * t_sets + o}, b, t_sets)
    over_sets = (loss_all, loss_grp, lg_send, lg_recv, lambda o: {"grp": o * t_sets + b}, a, i_sets)

    for j in range(t_count):
        texts.complete(j)
    image_pass(b, True)
    send_parts(*image_parts, b)
    for k in range(i_count):
        images.complete(k)
    for i in reversed(range(t_count)):
        text_pass(t_order[i])
        send_parts(*text_parts, t_order[i])
    for i in range(1, i_count):
        image_pass(i_order[i], False)
        send_parts(*image_parts, i_order[i])
    loss_out(jnp.full((8, 128), jnp.sum(loss_acc[...]), jnp.float32), *over_dev)

    def home_text(j, h):
        window = pl.ds(h * step_rows, step_rows)
        return remote(zs_t.at[j, window], zr_t.at[a, window], zt_send.at[j, h], zt_recv.at[a, h], {"grp": txt_group(j)})

    def home_image(k, h):
        window = pl.ds(h * step_rows, step_rows)
        return remote(zs_i.at[k, window], zr_i.at[b, window], zi_send.at[k, h], zi_recv.at[b, h], {"grp": img_group(k)})

    def reduce_text(i, h):
        window = pl.ds(h * step_rows, step_rows)
        j = t_order[i]
        total = sum_parts(*text_parts, j, h)
        if i:
            zs_t[j, window] = encode(total, unit)
            start(lambda: home_text(j, h))
            return

        @pl.when(t_own)
        def _():
            gt_ref[window] = total

        @pl.when(jnp.logical_not(t_own))
        def _():
            zs_t[j, window] = encode(total, unit)
            gt_ref[window] = jnp.zeros((step_rows, width), jnp.float32)

        start(lambda: home_text(j, h), jnp.logical_not(t_own))

    def reduce_image(k, h):
        window = pl.ds(h * step_rows, step_rows)
        zs_i[k, window] = encode(sum_parts(*image_parts, k, h), unit)
        start(lambda: home_image(k, h))

    for h in range(pieces):
        gi_ref[pl.ds(h * step_rows, step_rows)] = sum_parts(*image_parts, b, h)
    for i in reversed(range(1, t_count)):
        for h in range(pieces):
            reduce_text(i, h)
    loss_out(loss_in(*over_dev), *over_set)
    for i in range(1, i_count):
        for h in range(pieces):
            reduce_image(i_order[i], h)
    for h in range(pieces):
        reduce_text(0, h)
    loss_out(loss_in(*over_set), *over_sets)

    def land(ref, buf, sem, n, h):
        window = pl.ds(h * step_rows, step_rows)
        src = buf.at[n, window]
        remote(src, src, zi_send.at[0, 0], sem.at[n, h], {"dev": member(p, q, 1 - c)}).wait_recv()
        ref[window] = ref[window] + decode(buf[n, window], unit)

    for h in range(pieces):
        window = pl.ds(h * step_rows, step_rows)
        for i in range(1, i_count):
            land(gi_ref, zr_i, zi_recv, i_order[i], h)
        gi_ref[window] = multiplier * gi_ref[window]
    for h in range(pieces):
        window = pl.ds(h * step_rows, step_rows)
        for i in range(i_sets):
            pl.when(txt_target(i) != g)(functools.partial(land, gt_ref, zr_t, zt_recv, i, h))
        gt_ref[window] = multiplier * gt_ref[window]
    loss_ref[...] = loss_in(*over_sets) * (1.0 / (rows * members * groups))
    for make, when in started:
        if when is None:
            make().wait_send()
        else:
            pl.when(when)(lambda make=make: make().wait_send())


def write_out(gi_ref, gt_ref, loss_ref, gi_out, gt_out, loss_out):
    gi_out[...] = gi_ref[...]
    gt_out[...] = gt_ref[...]
    loss_out[0] = jnp.max(loss_ref[...])


def shards(groups, members, images, texts, logit_scale, logit_bias):
    rows, width = images.shape
    p_size, q_size = split_chips(members)
    i_sets, t_sets = split_groups(groups)
    i_count, t_count = t_sets, i_sets
    pieces = piece_count(rows)
    f32, bf16 = jnp.float32, jnp.bfloat16
    dma = pltpu.SemaphoreType.DMA
    unit = 2.0 ** math.floor(math.log2(4.9e7 / (1.05 * rows * members * groups)))

    def side_sems(n, targets, size):
        return [
            dma((n, size, CORES, pieces)),
            dma((targets, pieces)),
            dma((n, max(size - 1, 1), pieces)),
            dma((n, size, pieces)),
        ]

    scratch = [
        ((i_count, p_size, CORES, rows, width), bf16),
        ((t_count + 1, q_size, CORES, rows, width), bf16),
        ((i_count, p_size, rows, width), f32),
        ((t_count, q_size, rows, width), f32),
        ((i_count, max(p_size - 1, 1), rows, width), bf16),
        ((t_count, max(q_size - 1, 1), rows, width), bf16),
        ((i_count, p_size, rows, width), bf16),
        ((t_count, q_size, rows, width), bf16),
        ((i_count, rows, width), bf16),
        ((t_count, rows, width), bf16),
        ((i_count, rows, width), bf16),
        ((i_sets, rows, width), bf16),
        ((p_size * rows, t_count * q_size * CORES * rows), f32),
        ((8, 128), f32),
        ((members, 8, 128), f32),
        ((8, 128), f32),
        ((t_sets, 8, 128), f32),
        ((8, 128), f32),
        ((i_sets, 8, 128), f32),
    ]
    held = sum(math.prod(shape) * jnp.dtype(dtype).itemsize for shape, dtype in scratch)
    vmem, smem = pl.BlockSpec(memory_space=pltpu.VMEM), pl.BlockSpec(memory_space=pltpu.SMEM)
    grad_image, grad_text, loss = pl.pallas_call(
        functools.partial(kernel, t_sets, i_sets, p_size, q_size, pieces, unit),
        out_shape=(
            jax.ShapeDtypeStruct((rows, width), f32),
            jax.ShapeDtypeStruct((rows, width), f32),
            jax.ShapeDtypeStruct((8, 128), f32),
        ),
        in_specs=[pl.BlockSpec(memory_space=pl.ANY)] * 2 + [smem] * 2,
        out_specs=(vmem, vmem, vmem),
        scratch_shapes=[
            *(pltpu.VMEM(shape, dtype) for shape, dtype in scratch),
            *side_sems(i_count, i_count, p_size),
            *side_sems(t_count, i_sets, q_size),
            dma((i_count, max(p_size - 1, 1), pieces)), dma((i_count, p_size, pieces)),
            dma((t_count, max(q_size - 1, 1), pieces)), dma((t_count, q_size, pieces)),
            dma((i_count, pieces)), dma((i_count, pieces)),
            dma((t_count, pieces)), dma((i_sets, pieces)),
            dma((members,)), dma((members,)), dma((t_sets,)), dma((t_sets,)), dma((i_sets,)), dma((i_sets,)),
            dma((2,)),
        ],
        compiler_params=pltpu.CompilerParams(
            collective_id=0, has_side_effects=True, vmem_limit_bytes=min(held + (16 << 20), 60 << 20)
        ),
    )(*(pltpu.with_memory_space_constraint(x, pltpu.HBM) for x in (images, texts)), logit_scale, logit_bias)
    return pl.pallas_call(
        write_out,
        out_shape=(
            jax.ShapeDtypeStruct((rows, width), f32),
            jax.ShapeDtypeStruct((rows, width), f32),
            jax.ShapeDtypeStruct((1,), f32),
        ),
        in_specs=[vmem, vmem, vmem],
        out_specs=(vmem, vmem, smem),
        compiler_params=pltpu.CompilerParams(vmem_limit_bytes=4 << 20),
    )(grad_image, grad_text, loss)


def solution(mesh):
    in_specs = (P(("grp", "dev"), None), P(("grp", "dev"), None), P(), P())
    out_specs = (P(("grp", "dev"), None), P(("grp", "dev"), None), P())
    body = functools.partial(shards, mesh.shape["grp"], mesh.shape["dev"])
    return jax.shard_map(body, mesh=mesh, in_specs=in_specs, out_specs=out_specs, check_vma=False)
```

time: 43.6 us -> 41.3 us (0.947)
  Pallas kernels: 41.5 us -> 39.3 us
    pallas_call x1, Pallas kernels: 40.7 us -> 38.4 us  [shards(): pl.pallas_call(functools.partial(kernel, t_sets, i_sets, p_size, q_size,...]
where the time goes in v1:
time: 41.3 us; the launch traced here: 41.2 us
  Pallas kernels  39.3 us (95%)
  between operations  1.93 us (5%)
    pallas_call x1, Pallas kernels, shards(): pl.pallas_call(functools.partial(kernel, t_sets, i_sets, p_size, q_size,...  38.4 us
    pallas_call x1, Pallas kernels, shards(): pl.pallas_call(write_out, out_shape=(jax.ShapeDtypeStruct((rows, width),...  0.84 us

profile of v1, /device:TPU:0, one launch (start us, length us, event | category | flops | bytes accessed | tf_op | source)
XLA Modules:
  0.0 41.2 jit_solution(8187511814712506247)
XLA Ops:
  1.9 38.4 %shard_map.67 = (f32[48,1536]{1,0:T(8,128)S(1)}, f32[48,1536]{1,0:T(8,128)S(1)}, f32[8,128]{1,0:T(8,128)S(1)}) custom-call(bf16[48,1536]{1,0:T(8,128)(2,1)} %img_hbm.1, bf16[48,1536]{1,0:T(8,128)(2,1)} %txt_hbm.1, f32[1]{0:T(128)S(6)} %copy.7.scale_ref, f32[1]{0:T(128)S(6)} %copy.8.bias_ref), custom_call_target="tpu_custom_call" | custom-call | tf_op jit(solution)/shard_map/pallas_call | solution.py:439
  40.3 0.8 %shard_map.68 = (f32[48,1536]{1,0:T(8,128)}, f32[48,1536]{1,0:T(8,128)}, f32[1]{0:T(128)}) custom-call(f32[48,1536]{1,0:T(8,128)S(1)} %get-tuple-element.6.gi_ref, f32[48,1536]{1,0:T(8,128)S(1)} %get-tuple-element.7.gt_ref, f32[8,128]{1,0:T(8,128)S(1)} %get-tuple-element.8.loss_ref), custom_call_target="tpu_custom_call" | custom-call | tf_op jit(solution)/shard_map/pallas_call | solution.py:463

commit v2 on v1

v2 whole, which is shorter than its diff:
```python
import functools
import math

import jax
import jax.numpy as jnp
from jax import lax
from jax.experimental import pallas as pl
from jax.experimental.pallas import tpu as pltpu
from jax.sharding import PartitionSpec as P

MESH = pl.DeviceIdType.MESH
CORES = 2
POWER = 5


def split_chips(members):
    chips = members // CORES
    q_size = math.isqrt(chips)
    while chips % q_size:
        q_size -= 1
    return chips // q_size, q_size


def split_groups(groups):
    sets = math.isqrt(groups)
    while groups % sets:
        sets -= 1
    return sets, groups // sets


def piece_count(rows):
    for pieces in (3, 2):
        if rows % (16 * pieces) == 0:
            return pieces
    return 1


def pair_terms(logits, matched, losses):
    small = jnp.exp(-jnp.abs(logits))
    sigmoid = jnp.where(logits >= 0, 1.0, small) / (1.0 + small)
    weights = sigmoid - matched.astype(jnp.float32)
    if not losses:
        return weights, None
    signed = jnp.where(matched, -logits, logits)
    return weights, jnp.maximum(signed, 0.0) + jnp.log1p(small)


def encode(values, unit):
    scaled = values * unit
    square = scaled * scaled
    return (square * square * scaled).astype(jnp.bfloat16)


def decode(codes, unit):
    codes = codes.astype(jnp.float32)
    size = jnp.exp(jnp.log(jnp.abs(codes)) * (1.0 / POWER)) * (1.0 / unit)
    return jnp.where(codes < 0, -size, size)


def kernel(
    t_sets, i_sets, p_size, q_size, pieces, unit,
    img_hbm, txt_hbm, scale_ref, bias_ref,
    gi_ref, gt_ref, loss_ref,
    img_all, txt_all, acc_i, acc_t, code_i, code_t, part_i, part_t,
    zs_i, zs_t, zr_i, zr_t,
    loss_acc, loss_own, loss_dev, loss_sum, loss_set, loss_all, loss_grp,
    img_recv, img_both, img_z, img_plane, img_core,
    txt_recv, txt_both, txt_z, txt_plane, txt_core,
    pi_send, pi_recv, pt_send, pt_recv,
    zi_send, zi_recv, zt_send, zt_recv,
    loss_send, loss_recv,
    fetch_sem,
):
    rows, width = img_hbm.shape
    members = p_size * q_size * CORES
    i_count, t_count = t_sets, i_sets
    groups = i_sets * t_sets
    g = lax.axis_index("grp")
    d = lax.axis_index("dev")
    c = lax.rem(d, CORES)
    chip = d // CORES
    q = lax.rem(chip, q_size)
    p = chip // q_size
    a = g // t_sets
    b = lax.rem(g, t_sets)
    home = g // t_count
    step_rows = rows // pieces

    def member(pi, qi, ci):
        return (pi * q_size + qi) * CORES + ci

    def img_group(k):
        return a * i_count + k

    def txt_group(j):
        return b * t_count + j

    t_own = home == b
    t_slot = lax.rem(g, t_count)
    t_place = jnp.where(t_own, t_slot, t_count)
    below, above = home > b, home < b
    t_first = jnp.where(t_own, t_slot, jnp.where(below, t_count - 1, 0))
    t_turn = jnp.where(below, t_count - 1, 1)
    t_order = [lax.rem(t_first + i * t_turn, t_count) for i in range(t_count)]
    i_order = [lax.rem(b + i, i_count) for i in range(i_count)]

    waits = []

    def remote(src, dst, send, recv, target):
        return pltpu.make_async_remote_copy(
            src_ref=src, dst_ref=dst, send_sem=send, recv_sem=recv, device_id=target, device_id_type=MESH,
        )

    def at_end(make, when=None):
        waits.append((make, when))

    fetches = [
        pltpu.make_async_copy(src, dst, fetch_sem.at[i])
        for i, (src, dst) in enumerate((
            (txt_hbm, txt_all.at[t_place, q, c]), (img_hbm, img_all.at[b, p, c]),
        ))
    ]
    for fetch in fetches:
        fetch.start()
    barrier = pltpu.get_barrier_semaphore()

    def greet(axis, index):
        pl.semaphore_signal(barrier, inc=1, device_id={axis: index}, device_id_type=MESH)

    def txt_target(i):
        return i * t_sets + home

    awaited = (i_count - 1) + (p_size - 1) + (q_size - 1) + 1
    for i in range(1, i_count):
        greet("grp", img_group(i_order[i]))
    for j in range(t_count):
        pl.when(txt_group(j) != g)(functools.partial(lambda j: greet("grp", txt_group(j)), j))
    for i in range(i_sets):
        awaited = awaited + (txt_target(i) != g).astype(jnp.int32)
    for k in range(1, p_size):
        greet("dev", member(lax.rem(p + k, p_size), q, c))
    for k in range(1, q_size):
        greet("dev", member(p, lax.rem(q + k, q_size), c))
    greet("dev", member(p, q, 1 - c))
    pl.semaphore_wait(barrier, awaited)

    def from_core(ref, sem):
        remote(ref, ref, fetch_sem.at[0], sem, {"dev": member(p, q, 1 - c)}).wait_recv()

    def sent(ref, sem):
        remote(ref, ref, sem, fetch_sem.at[0], {"dev": member(p, q, 1 - c)}).wait_send()

    class Side:
        def __init__(self, all_ref, count, recv, both, plane, core, me, size, partner):
            self.all, self.count, self.recv, self.both = all_ref, count, recv, both
            self.plane, self.core = plane, core
            self.me, self.size, self.partner = me, size, partner
            for k in range(1, size):
                at_end(lambda k=k: sent(all_ref.at[pl.ds(0, count), me, c], plane.at[k - 1]))
            at_end(lambda: sent(all_ref.at[pl.ds(0, count), :, c], core.at[0]))

        def piece(self, n, m, cc, h):
            return self.all.at[n, m, cc, pl.ds(h * step_rows, step_rows)]

        def arrived(self, n, m, h):
            from_core(self.piece(n, m, c, h), self.recv.at[n, m, h])

        def out(self, n, m, h, send, target, source=None):
            ref = self.piece(n, m, c, h)
            src = ref if source is None else self.piece(source, m, c, h)
            return remote(src, ref, send, self.recv.at[n, m, h], target)

        def pass_on(self, n, m, h):
            ref = self.piece(n, m, c, h)
            remote(ref, ref, self.core.at[0], self.both.at[n], {"dev": member(p, q, 1 - c)}).start()

        def spread(self, n, h):
            for k in range(1, self.size):
                other = lax.rem(self.me + k, self.size)
                self.out(n, self.me, h, self.plane.at[k - 1], {"dev": self.partner(other)}).start()
            self.pass_on(n, self.me, h)

        def relay(self, n, h, own=None):
            if own is None:
                self.arrived(n, self.me, h)
            else:
                pl.when(jnp.logical_not(own))(lambda: self.arrived(n, self.me, h))
            self.spread(n, h)

        def relay_plane(self, n, h):
            for k in range(1, self.size):
                other = lax.rem(self.me + k, self.size)
                self.arrived(n, other, h)
                self.pass_on(n, other, h)

        def complete(self, n):
            from_core(self.all.at[n, :, 1 - c], self.both.at[n])

    texts = Side(txt_all, t_count, txt_recv, txt_both, txt_plane, txt_core, q, q_size, lambda o: member(p, o, c))
    images = Side(img_all, i_count, img_recv, img_both, img_plane, img_core, p, p_size, lambda o: member(o, q, c))

    fetches[1].wait()
    for h in range(pieces):
        for i in range(1, i_count):
            images.out(b, p, h, img_z.at[i - 1], {"grp": img_group(i_order[i])}).start()
        images.spread(b, h)
    for i in range(1, i_count):
        at_end(lambda i=i: sent(img_all.at[b, p, c], img_z.at[i - 1]))
    fetches[0].wait()
    for i in range(i_sets):
        @pl.when(txt_target(i) != g)
        def _():
            for h in range(pieces):
                texts.out(t_slot, q, h, txt_z.at[i], {"grp": txt_target(i)}, t_place).start()

        at_end(lambda i=i: sent(txt_all.at[t_place, q, c], txt_z.at[i]), txt_target(i) != g)
    multiplier = scale_ref[0]
    offset = bias_ref[0]

    last = pieces - 1
    near, rest = t_order[0], t_order[1:]
    for h in range(pieces):
        texts.relay(near, h, t_own)
        for k in i_order[1:]:
            images.relay(k, h)
    for h in range(pieces):
        images.relay_plane(b, h)
    for h in range(pieces):
        texts.relay_plane(near, h)
        for k in i_order[1:]:
            images.relay_plane(k, h)
        if h < last:
            for j in rest:
                texts.relay(j, h)

    def weigh(left, right, row_start, col_start, losses):
        logits = lax.dot_general(left, right, (((1,), (1,)), ((), ())), preferred_element_type=jnp.float32)
        logits = logits * multiplier + offset
        row = lax.broadcasted_iota(jnp.int32, logits.shape, 0) - row_start
        col = lax.broadcasted_iota(jnp.int32, logits.shape, 1) - col_start
        matched = (row == col) & (row >= 0) & (row < rows)
        weights, terms = pair_terms(logits, matched, losses)
        return jnp.dot(weights.astype(jnp.bfloat16), right, preferred_element_type=jnp.float32), terms

    far = 1 << 24

    def image_pass(j, first):
        left = img_all[:, :, c].reshape(i_count * p_size * rows, width)
        right = txt_all[j].reshape(q_size * CORES * rows, width)
        k = txt_group(j) - a * i_count
        col = jnp.where((k >= 0) & (k < i_count), (q * CORES + c) * rows, far)
        product, terms = weigh(left, right, (k * p_size + p) * rows, col, True)
        loss_acc[...] = terms if first else loss_acc[...] + terms
        product = product.reshape(i_count, p_size, rows, width)
        acc_i[...] = product if first else acc_i[...] + product

    def text_pass(j):
        left = txt_all[j, :, c].reshape(q_size * rows, width)
        right = img_all[...].reshape(i_count * p_size * CORES * rows, width)
        k = txt_group(j) - a * i_count
        col = jnp.where((k >= 0) & (k < i_count), ((k * p_size + p) * CORES + c) * rows, far)
        product, _ = weigh(left, right, q * rows, col, False)
        acc_t[j] = product.reshape(q_size, rows, width)

    def send_parts(acc, code, recv_buf, send, recv, side, n):
        for h in range(pieces):
            window = pl.ds(h * step_rows, step_rows)
            for k in range(1, side.size):
                other = lax.rem(side.me + k, side.size)
                code[n, k - 1, window] = encode(acc[n, other, window], unit)
                remote(
                    code.at[n, k - 1, window], recv_buf.at[n, side.me, window], send.at[k - 1], recv.at[n, k - 1, h],
                    {"dev": side.partner(other)},
                ).start()

    def sum_parts(acc, code, recv_buf, send, recv, side, n, h):
        window = pl.ds(h * step_rows, step_rows)
        total = acc[n, side.me, window]
        for k in range(1, side.size):
            other = lax.rem(side.me + k, side.size)
            from_core(recv_buf.at[n, other, window], recv.at[n, side.size - k - 1, h])
            total = total + decode(recv_buf[n, other, window], unit)
        return total

    image_parts = (acc_i, code_i, part_i, pi_send, pi_recv, images)
    text_parts = (acc_t, code_t, part_t, pt_send, pt_recv, texts)

    for acc, code, recv_buf, send, recv, side in (image_parts, text_parts):
        for k in range(1, side.size):
            at_end(lambda code=code, send=send, k=k: sent(code.at[:, k - 1], send.at[k - 1]))

    def loss_out(value, own, gathered, turn, target, me, size):
        own[...] = value
        gathered[0] = value
        for k in range(1, size):
            remote(own, gathered.at[size - k], loss_send.at[turn], loss_recv.at[turn], target(lax.rem(me + k, size))).start()
        if size > 1:
            at_end(lambda: sent(gathered.at[pl.ds(1, size - 1)], loss_send.at[turn]))

    def loss_in(own, gathered, turn, target, me, size):
        if size > 1:
            from_core(gathered.at[pl.ds(1, size - 1)], loss_recv.at[turn])
        return sum((gathered[k] for k in range(1, size)), gathered[0])

    over_dev = (loss_own, loss_dev, 0, lambda o: {"dev": o}, d, members)
    over_set = (loss_sum, loss_set, 1, lambda o: {"grp": a * t_sets + o}, b, t_sets)
    over_sets = (loss_all, loss_grp, 2, lambda o: {"grp": o * t_sets + b}, a, i_sets)

    for k in range(i_count):
        images.complete(k)
    texts.complete(near)
    for j in rest:
        texts.relay(j, last)
    text_pass(near)
    send_parts(*text_parts, near)
    for h in range(last):
        for j in rest:
            texts.relay_plane(j, h)
    image_pass(near, True)
    for j in rest:
        texts.relay_plane(j, last)
    for j in rest:
        texts.complete(j)
        image_pass(j, False)
    loss_out(jnp.full((8, 128), jnp.sum(loss_acc[...]), jnp.float32), *over_dev)
    for i in (*range(1, i_count), 0):
        send_parts(*image_parts, i_order[i])
    for j in reversed(rest):
        text_pass(j)
        send_parts(*text_parts, j)

    def home_text(j, h):
        window = pl.ds(h * step_rows, step_rows)
        return remote(zs_t.at[j, window], zr_t.at[a, window], zt_send.at[j], zt_recv.at[a, h], {"grp": txt_group(j)})

    def home_image(i, h):
        window = pl.ds(h * step_rows, step_rows)
        k = i_order[i]
        return remote(zs_i.at[k, window], zr_i.at[b, window], zi_send.at[i - 1], zi_recv.at[i - 1, h], {"grp": img_group(k)})

    for i in range(1, i_count):
        at_end(lambda i=i: sent(zs_i.at[i_order[i]], zi_send.at[i - 1]))
    for i in range(t_count):
        at_end(lambda j=t_order[i]: sent(zs_t.at[j], zt_send.at[j]), None if i else jnp.logical_not(t_own))

    def reduce_text(i, h):
        window = pl.ds(h * step_rows, step_rows)
        j = t_order[i]
        total = sum_parts(*text_parts, j, h)
        if i:
            zs_t[j, window] = encode(total, unit)
            home_text(j, h).start()
            return

        @pl.when(t_own)
        def _():
            gt_ref[window] = total

        @pl.when(jnp.logical_not(t_own))
        def _():
            zs_t[j, window] = encode(total, unit)
            gt_ref[window] = jnp.zeros((step_rows, width), jnp.float32)
            home_text(j, h).start()

    def reduce_image(i, h):
        window = pl.ds(h * step_rows, step_rows)
        k = i_order[i]
        zs_i[k, window] = encode(sum_parts(*image_parts, k, h), unit)
        home_image(i, h).start()

    for h in range(pieces):
        reduce_text(0, h)
    loss_out(loss_in(*over_dev), *over_set)
    for h in range(pieces):
        for i in range(1, i_count):
            reduce_image(i, h)
        for i in reversed(range(1, t_count)):
            reduce_text(i, h)
    loss_out(loss_in(*over_set), *over_sets)
    for h in range(pieces):
        gi_ref[pl.ds(h * step_rows, step_rows)] = sum_parts(*image_parts, b, h)

    def land(ref, buf, n, sem, h):
        window = pl.ds(h * step_rows, step_rows)
        from_core(buf.at[n, window], sem)
        ref[window] = ref[window] + decode(buf[n, window], unit)

    for h in range(pieces):
        window = pl.ds(h * step_rows, step_rows)
        for i in range(1, i_count):
            land(gi_ref, zr_i, i_order[i], zi_recv.at[i_count - i - 1, h], h)
        gi_ref[window] = multiplier * gi_ref[window]
        for i in range(i_sets):
            pl.when(txt_target(i) != g)(functools.partial(land, gt_ref, zr_t, i, zt_recv.at[i, h], h))
        gt_ref[window] = multiplier * gt_ref[window]
    loss_ref[...] = loss_in(*over_sets) * (1.0 / (rows * members * groups))
    for make, when in waits:
        if when is None:
            make()
        else:
            pl.when(when)(make)


def write_out(gi_ref, gt_ref, loss_ref, gi_out, gt_out, loss_out):
    gi_out[...] = gi_ref[...]
    gt_out[...] = gt_ref[...]
    loss_out[0] = jnp.max(loss_ref[...])


def shards(groups, members, images, texts, logit_scale, logit_bias):
    rows, width = images.shape
    p_size, q_size = split_chips(members)
    i_sets, t_sets = split_groups(groups)
    i_count, t_count = t_sets, i_sets
    pieces = piece_count(rows)
    f32, bf16 = jnp.float32, jnp.bfloat16
    dma = pltpu.SemaphoreType.DMA
    unit = 2.0 ** math.floor(math.log2(4.9e7 / (1.05 * rows * members * groups)))

    def side_sems(n, targets, size):
        return [dma((n, size, pieces)), dma((n,)), dma((max(targets, 1),)), dma((max(size - 1, 1),)), dma((1,))]

    def part_sems(n, size):
        return [dma((max(size - 1, 1),)), dma((n, max(size - 1, 1), pieces))]

    scratch = [
        ((i_count, p_size, CORES, rows, width), bf16),
        ((t_count + 1, q_size, CORES, rows, width), bf16),
        ((i_count, p_size, rows, width), f32),
        ((t_count, q_size, rows, width), f32),
        ((i_count, max(p_size - 1, 1), rows, width), bf16),
        ((t_count, max(q_size - 1, 1), rows, width), bf16),
        ((i_count, p_size, rows, width), bf16),
        ((t_count, q_size, rows, width), bf16),
        ((i_count, rows, width), bf16),
        ((t_count, rows, width), bf16),
        ((i_count, rows, width), bf16),
        ((i_sets, rows, width), bf16),
        ((i_count * p_size * rows, q_size * CORES * rows), f32),
        ((8, 128), f32),
        ((members, 8, 128), f32),
        ((8, 128), f32),
        ((t_sets, 8, 128), f32),
        ((8, 128), f32),
        ((i_sets, 8, 128), f32),
    ]
    held = sum(math.prod(shape) * jnp.dtype(dtype).itemsize for shape, dtype in scratch)
    vmem, smem = pl.BlockSpec(memory_space=pltpu.VMEM), pl.BlockSpec(memory_space=pltpu.SMEM)
    grad_image, grad_text, loss = pl.pallas_call(
        functools.partial(kernel, t_sets, i_sets, p_size, q_size, pieces, unit),
        out_shape=(
            jax.ShapeDtypeStruct((rows, width), f32),
            jax.ShapeDtypeStruct((rows, width), f32),
            jax.ShapeDtypeStruct((8, 128), f32),
        ),
        in_specs=[pl.BlockSpec(memory_space=pl.ANY)] * 2 + [smem] * 2,
        out_specs=(vmem, vmem, vmem),
        scratch_shapes=[
            *(pltpu.VMEM(shape, dtype) for shape, dtype in scratch),
            *side_sems(i_count, i_count - 1, p_size),
            *side_sems(t_count, i_sets, q_size),
            *part_sems(i_count, p_size),
            *part_sems(t_count, q_size),
            dma((max(i_count - 1, 1),)), dma((max(i_count - 1, 1), pieces)),
            dma((t_count,)), dma((i_sets, pieces)),
            dma((3,)), dma((3,)),
            dma((2,)),
        ],
        compiler_params=pltpu.CompilerParams(
            collective_id=0, has_side_effects=True, vmem_limit_bytes=min(held + (16 << 20), 60 << 20)
        ),
    )(*(pltpu.with_memory_space_constraint(x, pltpu.HBM) for x in (images, texts)), logit_scale, logit_bias)
    return pl.pallas_call(
        write_out,
        out_shape=(
            jax.ShapeDtypeStruct((rows, width), f32),
            jax.ShapeDtypeStruct((rows, width), f32),
            jax.ShapeDtypeStruct((1,), f32),
        ),
        in_specs=[vmem, vmem, vmem],
        out_specs=(vmem, vmem, smem),
        compiler_params=pltpu.CompilerParams(vmem_limit_bytes=4 << 20),
    )(grad_image, grad_text, loss)


def solution(mesh):
    in_specs = (P(("grp", "dev"), None), P(("grp", "dev"), None), P(), P())
    out_specs = (P(("grp", "dev"), None), P(("grp", "dev"), None), P())
    body = functools.partial(shards, mesh.shape["grp"], mesh.shape["dev"])
    return jax.shard_map(body, mesh=mesh, in_specs=in_specs, out_specs=out_specs, check_vma=False)
```

time: 41.3 us -> 34.8 us (0.84)
  Pallas kernels: 39.3 us -> 32.7 us
    pallas_call x1, Pallas kernels: 38.4 us -> 31.9 us  [shards(): pl.pallas_call(functools.partial(kernel, t_sets, i_sets, p_size, q_size,...]
where the time goes in v2:
time: 34.8 us; the launch traced here: 34.6 us
  Pallas kernels  32.7 us (94%)
  between operations  1.93 us (6%)
    pallas_call x1, Pallas kernels, shards(): pl.pallas_call(functools.partial(kernel, t_sets, i_sets, p_size, q_size,...  31.9 us
    pallas_call x1, Pallas kernels, shards(): pl.pallas_call(write_out, out_shape=(jax.ShapeDtypeStruct((rows, width),...  0.84 us

profile of v2, /device:TPU:0, one launch (start us, length us, event | category | flops | bytes accessed | tf_op | source)
XLA Modules:
  0.0 34.6 jit_solution(16287189892157452861)
XLA Ops:
  1.9 31.9 %shard_map.67 = (f32[48,1536]{1,0:T(8,128)S(1)}, f32[48,1536]{1,0:T(8,128)S(1)}, f32[8,128]{1,0:T(8,128)S(1)}) custom-call(bf16[48,1536]{1,0:T(8,128)(2,1)} %img_hbm.1, bf16[48,1536]{1,0:T(8,128)(2,1)} %txt_hbm.1, f32[1]{0:T(128)S(6)} %copy.7.scale_ref, f32[1]{0:T(128)S(6)} %copy.8.bias_ref), custom_call_target="tpu_custom_call" | custom-call | tf_op jit(solution)/shard_map/pallas_call | solution.py:449
  33.8 0.8 %shard_map.68 = (f32[48,1536]{1,0:T(8,128)}, f32[48,1536]{1,0:T(8,128)}, f32[1]{0:T(128)}) custom-call(f32[48,1536]{1,0:T(8,128)S(1)} %get-tuple-element.6.gi_ref, f32[48,1536]{1,0:T(8,128)S(1)} %get-tuple-element.7.gt_ref, f32[8,128]{1,0:T(8,128)S(1)} %get-tuple-element.8.loss_ref), custom_call_target="tpu_custom_call" | custom-call | tf_op jit(solution)/shard_map/pallas_call | solution.py:473
